TPU v7x, 512 devices: a whole 4x4x16 slice. The times are simulated.
512 devices in a mesh: ep: 64 (over x, z), tp: 8 (over y, core).
Axes of the slice: x: 4, y: 4, z: 16, core: 2. Of those that a mesh axis runs over, the one named last changes fastest.
Arguments:
- tokens: bfloat16 [1024, 4096], P('ep', 'tp'), may hold values from -6 to 6
- expert_ids: int32 [1024, 8], P('ep'), may hold values from 0 to 63, as said below
- route_weight: float32 [1024, 8], P('ep'), may hold values from 0.05 to 0.6
- gate_weight: bfloat16 [64, 1536, 4096], P('ep', 'tp'), may hold values from -0.09375 to 0.09375
- up_weight: bfloat16 [64, 1536, 4096], P('ep', 'tp'), may hold values from -0.09375 to 0.09375
- down_weight: bfloat16 [64, 1536, 4096], P('ep', 'tp'), may hold values from -0.21875 to 0.21875
Outputs:
- moe_out: bfloat16 [1024, 4096], P('ep', 'tp')
- act_absmax: float32 [2, 64], P(None, 'ep')
Inputs may be any that keep to these rules, and one draw needn't show every extreme that they name: `expert_ids`: each row names 8 different experts. Exactly 2 experts are named more than 2 times among the rows of one index of ep, in every such block, and at most 8 times; one of them is named exactly 8 times in every block, the other reaches 8 in some block. Every other expert is named at most 2 times among the rows of one index of ep, and one of them exactly 2 times in every block.
All inputs are finite; a program needn't handle non-finite values.
Results may differ from a plain program's by a relative error of at most 0.015.
Values may be sent and summed in bfloat16 or wider, within the bound.
No kernel may reach another device: no remote copies, remote signals or barrier semaphores. Data moves between devices by JAX's collectives and lax.ppermute only.
A program may use at most 64 MiB of HBM per device.

v0:
```python
import jax
import jax.numpy as jnp
from jax import lax
from jax.sharding import PartitionSpec as P

TOP = 8
EXP_DEV = 1


def copy_for_each(array, axis):
    count = lax.axis_size(axis)
    return lax.all_to_all(
        jnp.broadcast_to(array[None], (count, *array.shape)), axis, 0, 0, tiled=True
    )


def taken_together(array, axis):
    return copy_for_each(array, axis).max(axis=0)


def group_ranks(group_ids, group_total):
    onehot = (group_ids[:, None] == jnp.arange(group_total, dtype=jnp.int32)[None, :]).astype(
        jnp.int32
    )
    return jnp.sum((jnp.cumsum(onehot, axis=0) - 1) * onehot, axis=1)


def place_slots(slot_ids, valid, owner_row, slot_total):
    target = jnp.where(valid, slot_ids, slot_total)
    source = jnp.zeros((slot_total,), jnp.int32).at[target].set(owner_row, mode="drop")
    filled = jnp.zeros((slot_total,), jnp.bool_).at[target].set(True, mode="drop")
    return (source, filled)


def project_rows(row_block, weight):
    return lax.dot_general(
        row_block, weight, (((1,), (1,)), ((), ())), preferred_element_type=jnp.float32
    )


def serve_rows(row_block, gate_weight, up_weight, down_weight):
    senders, slot_count, feat_width = row_block.shape
    flat_rows = row_block.reshape(senders * slot_count, feat_width)
    gate_val = project_rows(flat_rows, gate_weight[0])
    up_val = project_rows(flat_rows, up_weight[0])
    hidden = (jax.nn.silu(gate_val) * up_val).astype(jnp.bfloat16)
    partial_value = jnp.dot(hidden, down_weight[0], preferred_element_type=jnp.float32)
    summed = lax.psum_scatter(
        partial_value.reshape(senders, slot_count, feat_width).astype(jnp.bfloat16),
        "tp",
        scatter_dimension=2,
        tiled=True,
    )
    returned_rows = lax.all_to_all(summed, "ep", split_axis=0, concat_axis=0, tiled=True)
    input_peak = (
        jnp.max(jnp.abs(flat_rows), axis=1).astype(jnp.float32).reshape(senders, slot_count)
    )
    hidden_peak = jnp.max(jnp.abs(hidden), axis=1).astype(jnp.float32).reshape(senders, slot_count)
    return (returned_rows, input_peak, hidden_peak)


def body(tokens, expert_ids, route_weight, gate_weight, up_weight, down_weight):
    senders = lax.axis_size("ep")
    experts = senders * EXP_DEV
    tok_rows = tokens.shape[0]
    common = tok_rows * TOP // experts
    hot_most = min(tok_rows, 4 * common)
    pick_ids = expert_ids.reshape(-1)
    owner_row = jnp.arange(pick_ids.shape[0], dtype=jnp.int32) // TOP
    zero_row = jnp.zeros((), jnp.bfloat16)
    rank_of = group_ranks(pick_ids, experts)
    send_slot = pick_ids * hot_most + rank_of
    source, filled = place_slots(
        send_slot, jnp.ones(pick_ids.shape, jnp.bool_), owner_row, experts * hot_most
    )
    outgoing = jnp.where(filled[:, None], tokens[source], zero_row).reshape(
        experts, hot_most, tokens.shape[1]
    )
    returned_rows, input_peak, hidden_peak = serve_rows(
        lax.all_gather(
            lax.all_to_all(outgoing, "ep", split_axis=0, concat_axis=0, tiled=True),
            "tp",
            axis=2,
            tiled=True,
        ),
        gate_weight,
        up_weight,
        down_weight,
    )
    out_table = returned_rows.reshape(experts * hot_most, returned_rows.shape[2])
    top_hidden = taken_together(jnp.max(hidden_peak), "tp")
    column = jnp.stack([jnp.max(input_peak), top_hidden])
    picked = out_table[send_slot].astype(jnp.float32).reshape(tok_rows, TOP, out_table.shape[1])
    moe_out = jnp.sum(picked * route_weight[:, :, None], axis=1).astype(jnp.bfloat16)
    act_absmax = column.reshape(2, 1)
    return (moe_out, act_absmax)


def solution(mesh):
    return jax.shard_map(
        body,
        mesh=mesh,
        in_specs=(
            P("ep", "tp"),
            P("ep", None),
            P("ep", None),
            P("ep", "tp", None),
            P("ep", "tp", None),
            P("ep", "tp", None),
        ),
        out_specs=(P("ep", "tp"), P(None, "ep")),
        check_vma=False,
    )
```

profile of v0, /device:TPU:31, one launch (start us, length us, event | category | flops | bytes accessed | tf_op | source)
XLA Modules:
  0.0 207.1 jit_solution(10847064991824207916)
XLA Ops:
  7.2 0.9 copy.21
  8.1 0.7 broadcast_multiply_fusion
  9.0 0.2 reduce_window_sum.11
  9.1 0.2 select_reduce_fusion
  9.5 1.0 scatter_custom_fusion.1
  10.5 1.0 scatter_custom_fusion
  11.6 2.7 %gather_fusion = bf16[512,512]{1,0:T(8,128)(2,1)S(1)} fusion(bf16[16,512]{1,0:T(8,128)(2,1)} %param.6, s32[1024]{0:T(1024)S(1)} %pad_clamp_fusion.1), kind=kCustom, calls=%fused_computation | custom fusion | bytes 1050624 | tf_op jit(solution)/shard_map/gather | solution.py:76
  14.3 0.1 bitcast_select_fusion
  14.5 47.8 %all_to_all.16 = bf16[64,8,512]{2,1,0:T(8,128)(2,1)} all-to-all(bf16[64,8,512]{2,1,0:T(8,128)(2,1)S(1)} %bitcast_select_fusion), channel_id=1, replica_groups=mesh['ep'=64,'tp'=8] {'ep'}, dimensions={0} | all-to-all | bytes 1048576 | tf_op jit(solution)/shard_map/all_to_all | solution.py:81
  62.4 33.3 %all-gather.2.cloned.1.call-done = bf16[64,8,4096]{2,1,0:T(8,128)(2,1)} async-done(((bf16[64,8,512]{2,1,0:T(8,128)(2,1)}), bf16[64,8,4096]{2,1,0:T(8,128)(2,1)}) %all-gather.2.cloned.1.call-update) | async-done | bytes 4194320 | tf_op jit(solution)/shard_map/all_gather | solution.py:80
  95.7 4.3 %fusion.2 = f32[512,192]{0,1:T(8,128)S(1)} fusion(bf16[64,8,4096]{2,1,0:T(8,128)(2,1)} %all-gather.2.cloned.1.call-done, bf16[1,192,4096]{2,1,0:T(8,128)(2,1)} %param.9), kind=kOutput, calls=%fused_computation.7 | convolution fusion | flops 805306368 | bytes 6160384 | tf_op jit(solution)/shard_map/dot_general | solution.py:36
  100.0 2.3 %abs_reduce_fusion.1 = (bf16[]{:T(256)}, bf16[512,192]{0,1:T(8,128)(2,1)S(1)}) fusion(bf16[1,192,4096]{2,1,0:T(8,128)(2,1)S(1)} %copy-done.3, bf16[64,8,4096]{2,1,0:T(8,128)(2,1)S(1)} %copy-done.1, f32[512,192]{0,1:T(8,128)S(1)} %fusion.2), kind=kOutput, calls=%fused_computation.19 | convolution fusion | flops 806092800 | bytes 6356994 | tf_op jit(solution)/shard_map/dot_general | solution.py:36
  102.3 0.1 copy.22
  102.4 3.2 %convolution_convert_fusion = bf16[64,8,4096]{2,1,0:T(8,128)(2,1)} fusion(bf16[1,192,4096]{2,1,0:T(8,128)(2,1)S(1)} %copy-done, bf16[512,192]{1,0:T(8,128)(2,1)S(1)} %copy.22), kind=kOutput, calls=%fused_computation.4 | convolution fusion | flops 807403520 | bytes 5963776 | tf_op jit(solution)/shard_map/dot_general | solution.py:47
  105.7 0.7 broadcast_in_dim.42
  106.3 8.0 %all_to_all.17 = f32[8,1,1]{2,1,0:T(1,128)S(1)} all-to-all(f32[8,1,1]{2,1,0:T(1,128)S(1)} %broadcast_in_dim.42), channel_id=1, replica_groups=mesh['ep'=64,'tp'=8] {'tp'}, dimensions={0} | all-to-all | bytes 64 | tf_op jit(solution)/shard_map/all_to_all | solution.py:12
  114.3 37.1 %reduce-scatter.2.cloned.1.call-done = bf16[64,8,512]{2,1,0:T(8,128)(2,1)} async-done(((bf16[64,8,4096]{2,1,0:T(8,128)(2,1)}), bf16[64,8,512]{2,1,0:T(8,128)(2,1)}) %reduce-scatter.2.cloned.1.call-update) | async-done | bytes 524304 | tf_op jit(solution)/shard_map/reduce_scatter | solution.py:48
  151.4 15.3 %all-to-all-start.1 = ((bf16[64,8,512]{2,1,0:T(8,128)(2,1)}), bf16[64,8,512]{2,1,0:T(8,128)(2,1)S(1)}, u32[]{:S(2)}, u32[]{:S(2)}) async-start(bf16[64,8,512]{2,1,0:T(8,128)(2,1)} %reduce-scatter.2.cloned.1.call-done), calls=%async_computation.2 | async-start | bytes 1048576 | tf_op jit(solution)/shard_map/all_to_all | solution.py:54
  166.9 3.4 %abs_reduce_fusion = bf16[]{:T(256)} fusion(bf16[64,8,4096]{2,1,0:T(8,128)(2,1)} %all-gather.2.cloned.1.call-done), kind=kLoop, calls=%fused_computation.9 | loop fusion | flops 4194303 | bytes 4194306 | tf_op jit(solution)/shard_map/reduce_max | solution.py:92
  170.9 0.6 reduce_max.46
  171.5 1.2 maximum_bitcast_fusion
  172.8 25.9 %all-to-all-done.1 = bf16[64,8,512]{2,1,0:T(8,128)(2,1)S(1)} async-done(((bf16[64,8,512]{2,1,0:T(8,128)(2,1)}), bf16[64,8,512]{2,1,0:T(8,128)(2,1)S(1)}, u32[]{:S(2)}, u32[]{:S(2)}) %all-to-all-start.1) | async-done | bytes 524320 | tf_op jit(solution)/shard_map/all_to_all | solution.py:54
  198.7 0.8 gather_fusion.1
  199.5 0.8 fusion.17
  (24 shorter events, 0.7 us)
Async XLA Ops:
  7.2 95.3 %copy-start = (bf16[1,192,4096]{2,1,0:T(8,128)(2,1)S(1)}, bf16[1,192,4096]{2,1,0:T(8,128)(2,1)}, u32[]{:S(2)}) copy-start(bf16[1,192,4096]{2,1,0:T(8,128)(2,1)} %param.11) | copy-start | bytes 4718596
  7.2 88.5 %all-gather.2.cloned.1.call-start = ((), (), s32[]{:S(2)}) async-start(), calls=%async_computation.4 | async-start | bytes 4718592 | tf_op jit(solution)/shard_map/all_gather | solution.py:80
  14.5 85.5 %copy-start.3 = (bf16[1,192,4096]{2,1,0:T(8,128)(2,1)S(1)}, bf16[1,192,4096]{2,1,0:T(8,128)(2,1)}, u32[]{:S(2)}) copy-start(bf16[1,192,4096]{2,1,0:T(8,128)(2,1)} %param.10) | copy-start | bytes 4718596
  62.3 89.1 %reduce-scatter.2.cloned.1.call-start = ((), (), s32[]{:S(2)}) async-start(), calls=%async_computation.5 | async-start | bytes 4718592 | tf_op jit(solution)/shard_map/reduce_scatter | solution.py:48
  95.7 4.4 %copy-start.1 = (bf16[64,8,4096]{2,1,0:T(8,128)(2,1)S(1)}, bf16[64,8,4096]{2,1,0:T(8,128)(2,1)}, u32[]{:S(2)}) copy-start(bf16[64,8,4096]{2,1,0:T(8,128)(2,1)} %all-gather.2.cloned.1.call-done) | copy-start | bytes 12582916
  102.4 64.4 %copy-start.2 = (f32[16,8]{0,1:T(8,128)S(1)}, f32[16,8]{0,1:T(8,128)}, u32[]{:S(2)}) copy-start(f32[16,8]{0,1:T(8,128)} %param.8) | copy-start | bytes 1540
  151.4 47.3 %all-to-all-start.1 = ((bf16[64,8,512]{2,1,0:T(8,128)(2,1)}), bf16[64,8,512]{2,1,0:T(8,128)(2,1)S(1)}, u32[]{:S(2)}, u32[]{:S(2)}) async-start(bf16[64,8,512]{2,1,0:T(8,128)(2,1)} %reduce-scatter.2.cloned.1.call-done), calls=%async_computation.2 | async-start | bytes 1048576 | tf_op jit(solution)/shard_map/all_to_all | solution.py:54
Sparse Core Ops, SparseCore 0:
  62.4 33.1 all-gather.1
  105.8 45.5 reduce-scatter.1
where the time goes:
time: 208 us; the launch traced here: 207 us
  waiting for transfers between devices  96.4 us (46%)
  blocking collectives  55.8 us (27%)
  starting transfers between devices  15.4 us (7%)
  between operations  14.9 us (7%)
  matrix products  9.82 us (5%)
  local copies, waits for them, and re-layouts  7.63 us (4%)
  other arithmetic  7.25 us (3%)
    all_to_all x1, blocking collectives, body(): lax.all_to_all(outgoing, 'ep', split_axis=0, concat_axis=0, tiled=True)  47.8 us
    reduce_scatter x1, waiting for transfers between devices, serve_rows(): lax.psum_scatter(partial_value.reshape(senders, slot_count, feat_width).a...  37.1 us
    all_gather x1, waiting for transfers between devices, body(): lax.all_gather(lax.all_to_all(outgoing, 'ep', split_axis=0, concat_axis=0...  33.3 us
    all_to_all x1, waiting for transfers between devices, serve_rows(): lax.all_to_all(summed, 'ep', split_axis=0, concat_axis=0, tiled=True)  25.9 us
    all_to_all x1, starting transfers between devices, serve_rows(): lax.all_to_all(summed, 'ep', split_axis=0, concat_axis=0, tiled=True)  15.3 us
    all_to_all x1, blocking collectives, copy_for_each(): lax.all_to_all(jnp.broadcast_to(array[None], (count, *array.shape)), axis...  7.96 us
    dot_general x2, matrix products, project_rows(): lax.dot_general(row_block, weight, (((1,), (1,)), ((), ())), preferred_el...  6.6 us
  transfers between devices with their start and end apart: 3, of which 3 were waited for; matrix products, arithmetic and copies ran while one was open for 3% of the time, Pallas kernels for 0%

commit v1 on v0

--- a/solution.py
+++ b/solution.py
@@ -2,9 +2,34 @@
 import jax.numpy as jnp
 from jax import lax
 from jax.sharding import PartitionSpec as P
+from jax.lax import axis_index, ppermute, psum
 
 TOP = 8
 EXP_DEV = 1
+
+
+def routes_all_define(sheet, d0):
+    net_axis = "tp"
+    left_arr = psum(1, net_axis)
+    f_now = axis_index(net_axis)
+    base_arr, reply, earlier = (left_arr, f_now, sheet.shape[d0])
+    trail = [b * base_arr if k0 == d0 else b for k0, b in enumerate(sheet.shape)]
+    mixed_arr = jnp.zeros(trail, sheet.dtype)
+    everything = res = sheet
+    local_part = lax.dynamic_update_slice_in_dim(mixed_arr, sheet, reply * earlier, axis=d0)
+    for i0 in range(1, base_arr // 2 + 1):
+        everything = ppermute(
+            everything, net_axis, [(k0, (k0 + 1) % base_arr) for k0 in range(base_arr)]
+        )
+        local_part = lax.dynamic_update_slice_in_dim(
+            local_part, everything, (reply - i0) % base_arr * earlier, axis=d0
+        )
+        if 2 * i0 < base_arr:
+            res = ppermute(res, net_axis, [(k0, (k0 - 1) % base_arr) for k0 in range(base_arr)])
+            local_part = lax.dynamic_update_slice_in_dim(
+                local_part, res, (reply + i0) % base_arr * earlier, axis=d0
+            )
+    return local_part
 
 
 def copy_for_each(array, axis):
@@ -77,11 +102,8 @@
         experts, hot_most, tokens.shape[1]
     )
     returned_rows, input_peak, hidden_peak = serve_rows(
-        lax.all_gather(
-            lax.all_to_all(outgoing, "ep", split_axis=0, concat_axis=0, tiled=True),
-            "tp",
-            axis=2,
-            tiled=True,
+        routes_all_define(
+            lax.all_to_all(outgoing, "ep", split_axis=0, concat_axis=0, tiled=True), 2
         ),
         gate_weight,
         up_weight,

time: 208 us -> 202 us (0.971)
  waiting for transfers between devices: 96.4 us -> 74.4 us
  starting transfers between devices: 15.4 us -> 29.9 us
  local copies, waits for them, and re-layouts: 7.63 us -> 11.2 us
  matrix products: 9.82 us -> 6.9 us
    all_gather x1 -> x0, waiting for transfers between devices: 33.3 us -> none  [body(): lax.all_gather(lax.all_to_all(outgoing, 'ep', split_axis=0, concat_axis=0...]
    ppermute x0 -> x7, waiting for transfers between devices: none -> 21 us  [the longest x4 21 us: routes_all_define(): ppermute(everything, net_axis, [(k0, (k0 + 1) % base_arr) for k0 in range...]
    ppermute x0 -> x7, starting transfers between devices: none -> 14.5 us  [the longest x4 14.3 us: routes_all_define(): ppermute(everything, net_axis, [(k0, (k0 + 1) % base_arr) for k0 in range...]
    reduce_scatter x1, waiting for transfers between devices: 37.1 us -> 27.4 us  [serve_rows(): lax.psum_scatter(partial_value.reshape(senders, slot_count, feat_width).a...]
    dot_general x2, matrix products: 6.6 us -> 3.68 us  [project_rows(): lax.dot_general(row_block, weight, (((1,), (1,)), ((), ())), preferred_el...]
    dynamic_update_slice x0 -> x8, local copies, waits for them, and re-layouts: none -> 2.6 us  [the longest x4 1.3 us: routes_all_define(): lax.dynamic_update_slice_in_dim(local_part, everything, (reply - i0) % ba...]
  transfers between devices with their start and end apart: 3 -> 9, of which waited for: 3 -> 6; matrix products, arithmetic and copies ran while one was open for 3% -> 4% of each run, Pallas kernels for 0% -> 0%
where the time goes in v1:
time: 202 us; the launch traced here: 201 us
  waiting for transfers between devices  74.4 us (37%)
  blocking collectives  56.5 us (28%)
  starting transfers between devices  29.9 us (15%)
  between operations  15 us (7%)
  local copies, waits for them, and re-layouts  11.2 us (6%)
  other arithmetic  7.25 us (4%)
  matrix products  6.9 us (3%)
    all_to_all x1, blocking collectives, body(): lax.all_to_all(outgoing, 'ep', split_axis=0, concat_axis=0, tiled=True)  47.6 us
    reduce_scatter x1, waiting for transfers between devices, serve_rows(): lax.psum_scatter(partial_value.reshape(senders, slot_count, feat_width).a...  27.4 us
    all_to_all x1, waiting for transfers between devices, serve_rows(): lax.all_to_all(summed, 'ep', split_axis=0, concat_axis=0, tiled=True)  25.9 us
    ppermute x4, waiting for transfers between devices, routes_all_define(): ppermute(everything, net_axis, [(k0, (k0 + 1) % base_arr) for k0 in range...  21 us
    all_to_all x1, starting transfers between devices, serve_rows(): lax.all_to_all(summed, 'ep', split_axis=0, concat_axis=0, tiled=True)  15.4 us
    ppermute x4, starting transfers between devices, routes_all_define(): ppermute(everything, net_axis, [(k0, (k0 + 1) % base_arr) for k0 in range...  14.3 us
    all_to_all x1, blocking collectives, copy_for_each(): lax.all_to_all(jnp.broadcast_to(array[None], (count, *array.shape)), axis...  8.97 us
  transfers between devices with their start and end apart: 9, of which 6 were waited for; matrix products, arithmetic and copies ran while one was open for 4% of the time, Pallas kernels for 0%

profile of v1, /device:TPU:31, one launch (start us, length us, event | category | flops | bytes accessed | tf_op | source)
XLA Modules:
  0.0 201.1 jit_solution(12177182204621807539)
XLA Ops:
  7.2 0.9 copy.21
  9.5 1.0 scatter_custom_fusion.1
  10.5 1.0 scatter_custom_fusion
  11.6 2.7 %gather_fusion = bf16[512,512]{1,0:T(8,128)(2,1)S(1)} fusion(bf16[16,512]{1,0:T(8,128)(2,1)} %param.6, s32[1024]{0:T(1024)S(1)} %pad_clamp_fusion.1), kind=kCustom, calls=%fused_computation | custom fusion | bytes 1050624 | tf_op jit(solution)/shard_map/gather | solution.py:101
  14.5 47.6 %all_to_all.16 = bf16[64,8,512]{2,1,0:T(8,128)(2,1)S(1)} all-to-all(bf16[64,8,512]{2,1,0:T(8,128)(2,1)S(1)} %bitcast_select_fusion), channel_id=1, replica_groups=mesh['ep'=64,'tp'=8] {'ep'}, dimensions={0} | all-to-all | bytes 1048576 | tf_op jit(solution)/shard_map/all_to_all | solution.py:106
  62.0 3.2 %collective-permute-start = (bf16[64,8,512]{2,1,0:T(8,128)(2,1)S(1)}, bf16[64,8,512]{2,1,0:T(8,128)(2,1)S(1)}, u32[]{:S(2)}, u32[]{:S(2)}) collective-permute-start(bf16[64,8,512]{2,1,0:T(8,128)(2,1)S(1)} %all_to_all.16), channel_id=1, source_target_pairs={{0,1},{1,2},{2,3},{3,4},{4,5},{5,6},{6,7},{7,0},{8,9},{9,10},{10,1... | collective-permute-start | bytes 1572872 | tf_op jit(solution)/shard_map/ppermute | solution.py:21
  65.4 5.9 %collective-permute-done = bf16[64,8,512]{2,1,0:T(8,128)(2,1)S(1)} collective-permute-done((bf16[64,8,512]{2,1,0:T(8,128)(2,1)S(1)}, bf16[64,8,512]{2,1,0:T(8,128)(2,1)S(1)}, u32[]{:S(2)}, u32[]{:S(2)}) %collective-permute-start) | collective-permute-done | bytes 524320 | tf_op jit(solution)/shard_map/ppermute | solution.py:21
  71.4 3.7 %collective-permute-start.2 = (bf16[64,8,512]{2,1,0:T(8,128)(2,1)S(1)}, bf16[64,8,512]{2,1,0:T(8,128)(2,1)}, u32[]{:S(2)}, u32[]{:S(2)}) collective-permute-start(bf16[64,8,512]{2,1,0:T(8,128)(2,1)S(1)} %collective-permute-done), channel_id=1, source_target_pairs={{0,1},{1,2},{2,3},{3,4},{4,5},{5,6},{6,7},{7,0},{8,9},{9,10},{10,1... | collective-permute-start | bytes 1572872 | tf_op jit(solution)/shard_map/ppermute | solution.py:21
  75.1 6.1 %collective-permute-done.2 = bf16[64,8,512]{2,1,0:T(8,128)(2,1)} collective-permute-done((bf16[64,8,512]{2,1,0:T(8,128)(2,1)S(1)}, bf16[64,8,512]{2,1,0:T(8,128)(2,1)}, u32[]{:S(2)}, u32[]{:S(2)}) %collective-permute-start.2) | collective-permute-done | bytes 524320 | tf_op jit(solution)/shard_map/ppermute | solution.py:21
  81.2 3.8 %collective-permute-start.4 = (bf16[64,8,512]{2,1,0:T(8,128)(2,1)}, bf16[64,8,512]{2,1,0:T(8,128)(2,1)S(1)}, u32[]{:S(2)}, u32[]{:S(2)}) collective-permute-start(bf16[64,8,512]{2,1,0:T(8,128)(2,1)} %collective-permute-done.2), channel_id=1, source_target_pairs={{0,1},{1,2},{2,3},{3,4},{4,5},{5,6},{6,7},{7,0},{8,9},{9,10},{10,1... | collective-permute-start | bytes 1572872 | tf_op jit(solution)/shard_map/ppermute | solution.py:21
  86.1 5.3 %collective-permute-done.4 = bf16[64,8,512]{2,1,0:T(8,128)(2,1)S(1)} collective-permute-done((bf16[64,8,512]{2,1,0:T(8,128)(2,1)}, bf16[64,8,512]{2,1,0:T(8,128)(2,1)S(1)}, u32[]{:S(2)}, u32[]{:S(2)}) %collective-permute-start.4) | collective-permute-done | bytes 524320 | tf_op jit(solution)/shard_map/ppermute | solution.py:21
  91.4 3.6 %collective-permute-start.6 = (bf16[64,8,512]{2,1,0:T(8,128)(2,1)S(1)}, bf16[64,8,512]{2,1,0:T(8,128)(2,1)S(1)}, u32[]{:S(2)}, u32[]{:S(2)}) collective-permute-start(bf16[64,8,512]{2,1,0:T(8,128)(2,1)S(1)} %collective-permute-done.4), channel_id=1, source_target_pairs={{0,1},{1,2},{2,3},{3,4},{4,5},{5,6},{6,7},{7,0},{8,9},{9,10},{10,1... | collective-permute-start | bytes 1572872 | tf_op jit(solution)/shard_map/ppermute | solution.py:21
  95.1 1.1 constant_dynamic-update-slice_fusion.3
  96.2 1.1 constant_dynamic-update-slice_fusion.2
  97.5 3.6 %collective-permute-done.6 = bf16[64,8,512]{2,1,0:T(8,128)(2,1)S(1)} collective-permute-done((bf16[64,8,512]{2,1,0:T(8,128)(2,1)S(1)}, bf16[64,8,512]{2,1,0:T(8,128)(2,1)S(1)}, u32[]{:S(2)}, u32[]{:S(2)}) %collective-permute-start.6) | collective-permute-done | bytes 524320 | tf_op jit(solution)/shard_map/ppermute | solution.py:21
  101.2 1.5 fusion.2
  102.8 2.1 %abs_reduce_fusion.1 = (bf16[]{:T(256)}, bf16[512,192]{0,1:T(8,128)(2,1)S(1)}) fusion(f32[512,192]{0,1:T(8,128)S(1)} %fusion.2, bf16[1,192,4096]{2,1,0:T(8,128)(2,1)S(1)} %copy-done.6, bf16[64,8,4096]{2,1,0:T(8,128)(2,1)S(1)} %constant_dynamic-update-slice_fusion.7), kind=kOutput, calls=%fused_computation.18 | convolution fusion | flops 806092800 | bytes 6356994 | tf_op jit(solution)/shard_map/dot_general | solution.py:61
  105.1 3.2 %convolution_convert_fusion = bf16[64,8,4096]{2,1,0:T(8,128)(2,1)} fusion(bf16[1,192,4096]{2,1,0:T(8,128)(2,1)S(1)} %copy-done, bf16[512,192]{1,0:T(8,128)(2,1)S(1)} %copy.22), kind=kOutput, calls=%fused_computation.4 | convolution fusion | flops 807403520 | bytes 5963776 | tf_op jit(solution)/shard_map/dot_general | solution.py:72
  109.0 9.0 %all_to_all.17 = f32[8,1,1]{2,1,0:T(1,128)S(1)} all-to-all(f32[8,1,1]{2,1,0:T(1,128)S(1)} %broadcast_in_dim.46), channel_id=1, replica_groups=mesh['ep'=64,'tp'=8] {'tp'}, dimensions={0} | all-to-all | bytes 64 | tf_op jit(solution)/shard_map/all_to_all | solution.py:37
  118.0 27.4 %reduce-scatter.2.cloned.1.call-done = bf16[64,8,512]{2,1,0:T(8,128)(2,1)} async-done(((bf16[64,8,4096]{2,1,0:T(8,128)(2,1)}), bf16[64,8,512]{2,1,0:T(8,128)(2,1)}) %reduce-scatter.2.cloned.1.call-update) | async-done | bytes 524304 | tf_op jit(solution)/shard_map/reduce_scatter | solution.py:73
  145.3 15.4 %all-to-all-start.1 = ((bf16[64,8,512]{2,1,0:T(8,128)(2,1)}), bf16[64,8,512]{2,1,0:T(8,128)(2,1)S(1)}, u32[]{:S(2)}, u32[]{:S(2)}) async-start(bf16[64,8,512]{2,1,0:T(8,128)(2,1)} %reduce-scatter.2.cloned.1.call-done), calls=%async_computation.2 | async-start | bytes 1048576 | tf_op jit(solution)/shard_map/all_to_all | solution.py:79
  160.8 3.4 %abs_reduce_fusion = bf16[]{:T(256)} fusion(bf16[64,8,4096]{2,1,0:T(8,128)(2,1)} %copy-done.1), kind=kLoop, calls=%fused_computation.9 | loop fusion | flops 4194303 | bytes 4194306 | tf_op jit(solution)/shard_map/reduce_max | solution.py:114
  165.5 1.2 maximum_bitcast_fusion
  166.7 25.9 %all-to-all-done.1 = bf16[64,8,512]{2,1,0:T(8,128)(2,1)S(1)} async-done(((bf16[64,8,512]{2,1,0:T(8,128)(2,1)}), bf16[64,8,512]{2,1,0:T(8,128)(2,1)S(1)}, u32[]{:S(2)}, u32[]{:S(2)}) %all-to-all-start.1) | async-done | bytes 524320 | tf_op jit(solution)/shard_map/all_to_all | solution.py:79
  (50 shorter events, 6.3 us)
Async XLA Ops:
  7.2 97.9 %copy-start = (bf16[1,192,4096]{2,1,0:T(8,128)(2,1)S(1)}, bf16[1,192,4096]{2,1,0:T(8,128)(2,1)}, u32[]{:S(2)}) copy-start(bf16[1,192,4096]{2,1,0:T(8,128)(2,1)} %param.11) | copy-start | bytes 4718596
  7.2 138.2 %reduce-scatter.2.cloned.1.call-start = ((), (), s32[]{:S(2)}) async-start(), calls=%async_computation.4 | async-start | bytes 4718592 | tf_op jit(solution)/shard_map/reduce_scatter | solution.py:73
  62.0 9.3 %collective-permute-start = (bf16[64,8,512]{2,1,0:T(8,128)(2,1)S(1)}, bf16[64,8,512]{2,1,0:T(8,128)(2,1)S(1)}, u32[]{:S(2)}, u32[]{:S(2)}) collective-permute-start(bf16[64,8,512]{2,1,0:T(8,128)(2,1)S(1)} %all_to_all.16), channel_id=1, source_target_pairs={{0,1},{1,2},{2,3},{3,4},{4,5},{5,6},{6,7},{7,0},{8,9},{9,10},{10,1... | collective-permute-start | bytes 1572872 | tf_op jit(solution)/shard_map/ppermute | solution.py:21
  65.3 9.8 %collective-permute-start.1 = (bf16[64,8,512]{2,1,0:T(8,128)(2,1)S(1)}, bf16[64,8,512]{2,1,0:T(8,128)(2,1)S(1)}, u32[]{:S(2)}, u32[]{:S(2)}) collective-permute-start(bf16[64,8,512]{2,1,0:T(8,128)(2,1)S(1)} %all_to_all.16), channel_id=1, source_target_pairs={{0,7},{1,0},{2,1},{3,2},{4,3},{5,4},{6,5},{7,6},{8,15},{9,8},{10,9... | collective-permute-start | bytes 1572872 | tf_op jit(solution)/shard_map/ppermute | solution.py:28
  71.4 3.7 %copy-start.2 = (bf16[64,8,512]{2,1,0:T(8,128)(2,1)}, bf16[64,8,512]{2,1,0:T(8,128)(2,1)S(1)}, u32[]{:S(2)}) copy-start(bf16[64,8,512]{2,1,0:T(8,128)(2,1)S(1)} %collective-permute-done) | copy-start | bytes 1572868
  71.4 9.8 %collective-permute-start.2 = (bf16[64,8,512]{2,1,0:T(8,128)(2,1)S(1)}, bf16[64,8,512]{2,1,0:T(8,128)(2,1)}, u32[]{:S(2)}, u32[]{:S(2)}) collective-permute-start(bf16[64,8,512]{2,1,0:T(8,128)(2,1)S(1)} %collective-permute-done), channel_id=1, source_target_pairs={{0,1},{1,2},{2,3},{3,4},{4,5},{5,6},{6,7},{7,0},{8,9},{9,10},{10,1... | collective-permute-start | bytes 1572872 | tf_op jit(solution)/shard_map/ppermute | solution.py:21
  75.1 10.5 %collective-permute-start.3 = (bf16[64,8,512]{2,1,0:T(8,128)(2,1)S(1)}, bf16[64,8,512]{2,1,0:T(8,128)(2,1)}, u32[]{:S(2)}, u32[]{:S(2)}) collective-permute-start(bf16[64,8,512]{2,1,0:T(8,128)(2,1)S(1)} %collective-permute-done.1), channel_id=1, source_target_pairs={{0,7},{1,0},{2,1},{3,2},{4,3},{5,4},{6,5},{7,6},{8,15},{9,8},{10,9... | collective-permute-start | bytes 1572872 | tf_op jit(solution)/shard_map/ppermute | solution.py:28
  81.2 10.2 %collective-permute-start.4 = (bf16[64,8,512]{2,1,0:T(8,128)(2,1)}, bf16[64,8,512]{2,1,0:T(8,128)(2,1)S(1)}, u32[]{:S(2)}, u32[]{:S(2)}) collective-permute-start(bf16[64,8,512]{2,1,0:T(8,128)(2,1)} %collective-permute-done.2), channel_id=1, source_target_pairs={{0,1},{1,2},{2,3},{3,4},{4,5},{5,6},{6,7},{7,0},{8,9},{9,10},{10,1... | collective-permute-start | bytes 1572872 | tf_op jit(solution)/shard_map/ppermute | solution.py:21
  85.0 1.0 copy-start.3
  85.5 15.7 %copy-start.5 = (bf16[1,192,4096]{2,1,0:T(8,128)(2,1)S(1)}, bf16[1,192,4096]{2,1,0:T(8,128)(2,1)}, u32[]{:S(2)}) copy-start(bf16[1,192,4096]{2,1,0:T(8,128)(2,1)} %param.9) | copy-start | bytes 4718596
  85.6 11.8 %collective-permute-start.5 = (bf16[64,8,512]{2,1,0:T(8,128)(2,1)}, bf16[64,8,512]{2,1,0:T(8,128)(2,1)S(1)}, u32[]{:S(2)}, u32[]{:S(2)}) collective-permute-start(bf16[64,8,512]{2,1,0:T(8,128)(2,1)} %collective-permute-done.3), channel_id=1, source_target_pairs={{0,7},{1,0},{2,1},{3,2},{4,3},{5,4},{6,5},{7,6},{8,15},{9,8},{10,9... | collective-permute-start | bytes 1572872 | tf_op jit(solution)/shard_map/ppermute | solution.py:28
  91.4 9.7 %collective-permute-start.6 = (bf16[64,8,512]{2,1,0:T(8,128)(2,1)S(1)}, bf16[64,8,512]{2,1,0:T(8,128)(2,1)S(1)}, u32[]{:S(2)}, u32[]{:S(2)}) collective-permute-start(bf16[64,8,512]{2,1,0:T(8,128)(2,1)S(1)} %collective-permute-done.4), channel_id=1, source_target_pairs={{0,1},{1,2},{2,3},{3,4},{4,5},{5,6},{6,7},{7,0},{8,9},{9,10},{10,1... | collective-permute-start | bytes 1572872 | tf_op jit(solution)/shard_map/ppermute | solution.py:21
  97.4 5.4 %copy-start.6 = (bf16[1,192,4096]{2,1,0:T(8,128)(2,1)S(1)}, bf16[1,192,4096]{2,1,0:T(8,128)(2,1)}, u32[]{:S(2)}) copy-start(bf16[1,192,4096]{2,1,0:T(8,128)(2,1)} %param.10) | copy-start | bytes 4718596
  101.2 3.7 %copy-start.1 = (bf16[64,8,4096]{2,1,0:T(8,128)(2,1)}, bf16[64,8,4096]{2,1,0:T(8,128)(2,1)S(1)}, u32[]{:S(2)}) copy-start(bf16[64,8,4096]{2,1,0:T(8,128)(2,1)S(1)} %constant_dynamic-update-slice_fusion.7) | copy-start | bytes 12582916
  105.1 55.6 %copy-start.4 = (f32[16,8]{0,1:T(8,128)S(1)}, f32[16,8]{0,1:T(8,128)}, u32[]{:S(2)}) copy-start(f32[16,8]{0,1:T(8,128)} %param.8) | copy-start | bytes 1540
  145.3 47.3 %all-to-all-start.1 = ((bf16[64,8,512]{2,1,0:T(8,128)(2,1)}), bf16[64,8,512]{2,1,0:T(8,128)(2,1)S(1)}, u32[]{:S(2)}, u32[]{:S(2)}) async-start(bf16[64,8,512]{2,1,0:T(8,128)(2,1)} %reduce-scatter.2.cloned.1.call-done), calls=%async_computation.2 | async-start | bytes 1048576 | tf_op jit(solution)/shard_map/all_to_all | solution.py:79
Sparse Core Ops, SparseCore 0:
  108.5 36.8 reduce-scatter.1
